TPU v7x, 32 devices: a whole 2x2x4 slice. The times are simulated.
32 devices in a mesh: rows: 8 (over y, x, core), hub: 4 (over z).
Axes of the slice: x: 2, y: 2, z: 4, core: 2. Of those that a mesh axis runs over, the one named last changes fastest.
Arguments:
- tail_blocks: float32 [2304, 128, 128], P(('rows', 'hub')), may hold values from -0.21875 to 0.21875
- tail_row: int32 [2304], P(('rows', 'hub')), may hold values from 0 to 15
- tail_owner: int32 [2304, 1], P(('rows', 'hub')), may hold values from 0 to 7; in each aligned block of 72 rows (0 to 71, 72 to 143, ...) at most 27 rows name the same one
- tail_slot: int32 [2304], P(('rows', 'hub')), may hold values from 0 to 63
- hub_blocks: float32 [768, 128, 128], P(('rows', 'hub')), may hold values from -0.21875 to 0.21875
- hub_row: int32 [768], P(('rows', 'hub')), may hold values from 0 to 15
- hub_col: int32 [768], P(('rows', 'hub')), may hold values from 0 to 127
- x_tail: float32 [2048, 128], P(('rows', 'hub')), may hold values from 0 to 0.5
- cost_tail: float32 [2048, 128], P(('rows', 'hub')), may hold values from -6 to 6
- upper_tail: float32 [2048, 128], P(('rows', 'hub')), may hold values from 0.5 to 2
- x_hub: float32 [128, 128], P('hub'), may hold values from 0 to 0.5
- cost_hub: float32 [128, 128], P('hub'), may hold values from -6 to 6
- upper_hub: float32 [128, 128], P('hub'), may hold values from 0.5 to 2
- duals: float32 [512, 128], P(('rows', 'hub')), may hold values from 0 to 1
- demand: float32 [512, 128], P(('rows', 'hub')), may hold values from -6 to 6
Outputs:
- x_tail_out: float32 [2048, 128], P(('rows', 'hub'))
- x_hub_out: float32 [128, 128], P('hub')
- duals_out: float32 [512, 128], P(('rows', 'hub'))
Inputs may be any that keep to these rules, and one draw needn't show every extreme that they name: `tail_owner`: among the blocks of one device no owner is named more than 27 times; on some device one owner is named exactly 27 times.
All inputs are finite; a program needn't handle non-finite values.
Results may differ from a plain program's by a relative error of at most 0.0001.
Values sent between devices are 32-bit elements; how exact they have to be, the bound alone decides.
No kernel may reach another device: no remote copies, remote signals or barrier semaphores. Data moves between devices by JAX's collectives and lax.ppermute only.
A program may use at most 64 MiB of HBM per device.

v0:
```python
import jax
import jax.numpy as jnp
from jax import lax
from jax.sharding import PartitionSpec as P

ITERS = 3
primal_step = 0.25
dual_step = 0.25


def on_device(
    tail_blocks,
    tail_row,
    tail_owner,
    tail_slot,
    hub_blocks,
    hub_row,
    hub_col,
    x_tail,
    cost_tail,
    upper_tail,
    x_hub,
    cost_hub,
    upper_hub,
    duals,
    demand,
):
    highest = lax.Precision.HIGHEST
    row_devs = lax.axis_size("rows")
    hub_devs = lax.axis_size("hub")
    tail_count = tail_blocks.shape[0]
    col_blocks = x_tail.shape[0]
    row_blocks = duals.shape[0]
    hub_share = x_hub.shape[0]
    hub_total = hub_share * hub_devs
    width = x_tail.shape[1]
    capacity = max(2, 3 * tail_count // row_devs)
    owners = tail_owner[:, 0]
    hits = (owners[:, None] == jnp.arange(row_devs, dtype=jnp.int32)[None, :]).astype(jnp.int32)
    within = jnp.sum(jnp.cumsum(hits, axis=0) * hits, axis=1) - 1
    places = owners * capacity + within
    asked_slots = jnp.zeros((row_devs * capacity,), jnp.int32).at[places].set(tail_slot)
    requested = lax.all_to_all(
        asked_slots.reshape(row_devs, capacity), "rows", split_axis=0, concat_axis=0, tiled=True
    ).reshape(-1)
    collector = (jnp.arange(col_blocks, dtype=jnp.int32)[:, None] == requested[None, :]).astype(
        jnp.float32
    )
    tail_rowpick = (jnp.arange(row_blocks, dtype=jnp.int32)[:, None] == tail_row[None, :]).astype(
        jnp.float32
    )
    hub_rowpick = (jnp.arange(row_blocks, dtype=jnp.int32)[:, None] == hub_row[None, :]).astype(
        jnp.float32
    )
    hub_state = x_hub
    hub_pick = (jnp.arange(hub_total, dtype=jnp.int32)[:, None] == hub_col[None, :]).astype(
        jnp.float32
    )
    tail_state = x_tail
    for iteration in range(ITERS):
        tail_terms = jnp.einsum("bij,bi->bj", tail_blocks, duals[tail_row], precision=highest)
        outgoing = jnp.zeros((row_devs * capacity, width), jnp.float32).at[places].set(tail_terms)
        arrived = lax.all_to_all(
            outgoing.reshape(row_devs, capacity, width),
            "rows",
            split_axis=0,
            concat_axis=0,
            tiled=True,
        )
        tail_image = jnp.dot(
            collector,
            arrived.reshape(-1, width),
            precision=highest,
            preferred_element_type=jnp.float32,
        )
        tail_next = jnp.minimum(
            jnp.maximum(tail_state - primal_step * (cost_tail - tail_image), 0.0), upper_tail
        )
        tail_extra = 2.0 * tail_next - tail_state
        hub_terms = jnp.einsum("bij,bi->bj", hub_blocks, duals[hub_row], precision=highest)
        hub_partial = jnp.dot(
            hub_pick, hub_terms, precision=highest, preferred_element_type=jnp.float32
        )
        hub_sums = lax.psum_scatter(hub_partial, "hub", scatter_dimension=0, tiled=True)
        hub_sums = lax.psum(hub_sums, "rows")
        hub_next = jnp.minimum(
            jnp.maximum(hub_state - primal_step * (cost_hub - hub_sums), 0.0), upper_hub
        )
        hub_extra = 2.0 * hub_next - hub_state
        hub_full = lax.all_gather(hub_extra, "hub", axis=0, tiled=True)
        gathered = lax.all_gather(tail_extra, "rows", axis=0, tiled=True)
        tail_picked = gathered[owners * col_blocks + tail_slot]
        tail_product = jnp.einsum("bij,bj->bi", tail_blocks, tail_picked, precision=highest)
        hub_product = jnp.einsum("bij,bj->bi", hub_blocks, hub_full[hub_col], precision=highest)
        primal_image = jnp.dot(
            tail_rowpick, tail_product, precision=highest, preferred_element_type=jnp.float32
        )
        primal_image = primal_image + jnp.dot(
            hub_rowpick, hub_product, precision=highest, preferred_element_type=jnp.float32
        )
        duals = jnp.maximum(duals + dual_step * (demand - primal_image), 0.0)
        tail_state = tail_next
        hub_state = hub_next
    return (tail_state, hub_state, duals)


def solution(mesh):
    in_specs = (
        P(("rows", "hub"), None, None),
        P(("rows", "hub")),
        P(("rows", "hub"), None),
        P(("rows", "hub")),
        P(("rows", "hub"), None, None),
        P(("rows", "hub")),
        P(("rows", "hub")),
        P(("rows", "hub"), None),
        P(("rows", "hub"), None),
        P(("rows", "hub"), None),
        P("hub", None),
        P("hub", None),
        P("hub", None),
        P(("rows", "hub"), None),
        P(("rows", "hub"), None),
    )
    out_specs = (P(("rows", "hub"), None), P("hub", None), P(("rows", "hub"), None))
    return jax.shard_map(
        on_device, mesh=mesh, in_specs=in_specs, out_specs=out_specs, check_vma=False
    )
```

profile of v0, /device:TPU:0, one launch (start us, length us, event | category | flops | bytes accessed | tf_op | source)
XLA Modules:
  0.0 261.1 jit_solution(8980955782605521598)
XLA Ops:
  7.2 0.8 fusion.33
  8.2 0.8 select_reduce_fusion
  9.0 0.7 fusion.49
  9.7 0.9 scatter_custom_fusion
  10.6 0.7 all_to_all.15
  11.3 5.2 %all-to-all-start = ((s32[8,1,27]{2,1,0:T(1,128)}), s32[8,1,27]{2,1,0:T(1,128)S(1)}, u32[]{:S(2)}, u32[]{:S(2)}) async-start(s32[8,1,27]{2,1,0:T(1,128)} %all_to_all.15), calls=%async_computation | async-start | bytes 8192 | tf_op jit(solution)/shard_map/all_to_all | solution.py:43
  16.5 0.7 compare_select_fusion.1
  17.2 1.3 gather_fusion.2
  18.5 1.4 fusion.54
  19.9 1.5 fusion.26
  21.4 0.7 compare_select_fusion.2
  22.1 0.7 compare_select_fusion
  22.7 0.7 compare_select_fusion.3
  23.4 1.3 gather_fusion
  24.7 5.8 %fusion.52 = f32[72,1,128]{2,1,0:T(1,128)S(1)} fusion(f32[72,128,1]{1,2,0:T(1,128)S(1)} %bitcast.112, f32[72,128,128]{2,1,0:T(8,128)} %param.15), kind=kOutput, calls=%fused_computation.99 | convolution fusion | flops 14155776 | bytes 4792320 | tf_op jit(solution)/shard_map/bij,bi->bj/dot_general | solution.py:61
  30.6 0.8 scatter_custom_fusion.1
  31.3 0.7 reshape.42
  32.0 4.2 %all-to-all-start.1 = ((f32[8,27,128]{2,1,0:T(8,128)}), f32[8,27,128]{2,1,0:T(8,128)S(1)}, u32[]{:S(2)}, u32[]{:S(2)}) async-start(f32[8,27,128]{2,1,0:T(8,128)} %reshape.42), calls=%async_computation.1 | async-start | bytes 262144 | tf_op jit(solution)/shard_map/all_to_all | solution.py:63
  36.2 0.5 broadcast.172
  36.7 0.7 reduce.3
  37.4 4.2 %all-to-all-done.1 = f32[8,27,128]{2,1,0:T(8,128)S(1)} async-done(((f32[8,27,128]{2,1,0:T(8,128)}), f32[8,27,128]{2,1,0:T(8,128)S(1)}, u32[]{:S(2)}, u32[]{:S(2)}) %all-to-all-start.1) | async-done | bytes 110624 | tf_op jit(solution)/shard_map/all_to_all | solution.py:63
  41.7 0.2 multiply_subtract_fusion.2
  41.9 8.4 %all_gather.18 = f32[512,128]{1,0:T(8,128)S(1)} all-gather(f32[64,128]{1,0:T(8,128)S(1)} %get-tuple-element.9), channel_id=1, replica_groups=mesh['rows'=8,'hub'=4] {'rows'}, dimensions={0}, use_global_device_ids=true | all-gather | bytes 294912 | tf_op jit(solution)/shard_map/all_gather | solution.py:91
  50.3 0.6 gather_fusion.1
  50.9 9.2 %fusion.53 = f32[72,1,128]{2,1,0:T(1,128)S(1)} fusion(f32[72,128,1]{1,2,0:T(1,128)S(1)} %bitcast.109, f32[72,128,128]{2,1,0:T(8,128)} %param.15), kind=kOutput, calls=%fused_computation.100 | convolution fusion | flops 14155776 | bytes 4792320 | tf_op jit(solution)/shard_map/bij,bj->bi/dot_general | solution.py:93
  60.2 23.7 %psum.21 = f32[32,128]{1,0:T(8,128)S(1)} all-reduce(f32[32,128]{1,0:T(8,128)} %reduce-scatter.4.cloned.1.call-done), channel_id=1, replica_groups=mesh['rows'=8,'hub'=4] {'rows'}, use_global_device_ids=true, to_apply=%region_5.6 | all-reduce | flops 4096 | bytes 32768 | tf_op jit(solution)/shard_map/psum | solution.py:85
  84.0 13.6 %all_gather.19 = f32[128,128]{1,0:T(8,128)S(1)} all-gather(f32[32,128]{1,0:T(8,128)S(1)} %get-tuple-element.7), channel_id=1, replica_groups=mesh['rows'=8,'hub'=4] {'hub'}, dimensions={0}, use_global_device_ids=true | all-gather | bytes 81920 | tf_op jit(solution)/shard_map/all_gather | solution.py:90
  97.6 0.6 gather_fusion.3
  98.1 2.5 fusion.55
  100.8 0.6 gather_fusion.4
  101.4 0.6 gather_fusion.6
  102.0 5.8 %fusion.56 = f32[72,1,128]{2,1,0:T(1,128)S(1)} fusion(f32[72,128,1]{1,2,0:T(1,128)S(1)} %bitcast.110, f32[72,128,128]{2,1,0:T(8,128)} %param.15), kind=kOutput, calls=%fused_computation.103 | convolution fusion | flops 14155776 | bytes 4792320 | tf_op jit(solution)/shard_map/bij,bi->bj/dot_general | solution.py:61
  107.8 0.8 scatter_custom_fusion.2
  108.6 0.7 reshape.44
  109.2 3.4 %all-to-all-start.2 = ((f32[8,27,128]{2,1,0:T(8,128)}), f32[8,27,128]{2,1,0:T(8,128)S(1)}, u32[]{:S(2)}, u32[]{:S(2)}) async-start(f32[8,27,128]{2,1,0:T(8,128)} %reshape.44), calls=%async_computation.3 | async-start | bytes 262144 | tf_op jit(solution)/shard_map/all_to_all | solution.py:63
  112.7 1.4 fusion.58
  114.1 0.8 fusion.25
  115.0 3.2 %all-to-all-done.2 = f32[8,27,128]{2,1,0:T(8,128)S(1)} async-done(((f32[8,27,128]{2,1,0:T(8,128)}), f32[8,27,128]{2,1,0:T(8,128)S(1)}, u32[]{:S(2)}, u32[]{:S(2)}) %all-to-all-start.2) | async-done | bytes 110624 | tf_op jit(solution)/shard_map/all_to_all | solution.py:63
  118.4 8.4 %all_gather.20 = f32[512,128]{1,0:T(8,128)S(1)} all-gather(f32[64,128]{1,0:T(8,128)S(1)} %get-tuple-element.11), channel_id=1, replica_groups=mesh['rows'=8,'hub'=4] {'rows'}, dimensions={0}, use_global_device_ids=true | all-gather | bytes 294912 | tf_op jit(solution)/shard_map/all_gather | solution.py:91
  126.7 0.6 gather_fusion.5
  127.3 9.2 %fusion.57 = f32[72,1,128]{2,1,0:T(1,128)S(1)} fusion(f32[72,128,1]{1,2,0:T(1,128)S(1)} %bitcast.111, f32[72,128,128]{2,1,0:T(8,128)} %param.15), kind=kOutput, calls=%fused_computation.104 | convolution fusion | flops 14155776 | bytes 4792320 | tf_op jit(solution)/shard_map/bij,bj->bi/dot_general | solution.py:93
  136.7 23.6 %psum.22 = f32[32,128]{1,0:T(8,128)S(1)} all-reduce(f32[32,128]{1,0:T(8,128)} %reduce-scatter.6.cloned.1.call-done), channel_id=1, replica_groups=mesh['rows'=8,'hub'=4] {'rows'}, use_global_device_ids=true, to_apply=%region_8.9 | all-reduce | flops 4096 | bytes 32768 | tf_op jit(solution)/shard_map/psum | solution.py:85
  160.3 13.4 %all_gather.21 = f32[128,128]{1,0:T(8,128)S(1)} all-gather(f32[32,128]{1,0:T(8,128)S(1)} %get-tuple-element.5), channel_id=1, replica_groups=mesh['rows'=8,'hub'=4] {'hub'}, dimensions={0}, use_global_device_ids=true | all-gather | bytes 81920 | tf_op jit(solution)/shard_map/all_gather | solution.py:90
  173.6 0.6 gather_fusion.7
  174.2 2.5 fusion.59
  176.9 0.6 gather_fusion.8
  177.5 0.6 gather_fusion.9
  178.1 5.8 %fusion.60 = f32[72,1,128]{2,1,0:T(1,128)S(1)} fusion(f32[72,128,1]{1,2,0:T(1,128)S(1)} %bitcast.107, f32[72,128,128]{2,1,0:T(8,128)} %param.15), kind=kOutput, calls=%fused_computation.107 | convolution fusion | flops 14155776 | bytes 4792320 | tf_op jit(solution)/shard_map/bij,bi->bj/dot_general | solution.py:61
  183.9 0.8 scatter_custom_fusion.3
  184.6 0.7 reshape.46
  185.3 3.4 %all-to-all-start.3 = ((f32[8,27,128]{2,1,0:T(8,128)}), f32[8,27,128]{2,1,0:T(8,128)S(1)}, u32[]{:S(2)}, u32[]{:S(2)}) async-start(f32[8,27,128]{2,1,0:T(8,128)} %reshape.46), calls=%async_computation.5 | async-start | bytes 262144 | tf_op jit(solution)/shard_map/all_to_all | solution.py:63
  188.8 1.4 fusion.61
  190.2 0.8 fusion.24
  191.0 3.2 %all-to-all-done.3 = f32[8,27,128]{2,1,0:T(8,128)S(1)} async-done(((f32[8,27,128]{2,1,0:T(8,128)}), f32[8,27,128]{2,1,0:T(8,128)S(1)}, u32[]{:S(2)}, u32[]{:S(2)}) %all-to-all-start.3) | async-done | bytes 110624 | tf_op jit(solution)/shard_map/all_to_all | solution.py:63
  194.2 0.8 multiply_subtract_fusion
  195.1 8.3 %all_gather.22 = f32[512,128]{1,0:T(8,128)S(1)} all-gather(f32[64,128]{1,0:T(8,128)S(1)} %get-tuple-element.13), channel_id=1, replica_groups=mesh['rows'=8,'hub'=4] {'rows'}, dimensions={0}, use_global_device_ids=true | all-gather | bytes 294912 | tf_op jit(solution)/shard_map/all_gather | solution.py:91
  203.4 0.6 gather_fusion.10
  204.0 9.2 %fusion.62 = f32[72,1,128]{2,1,0:T(1,128)S(1)} fusion(f32[72,128,1]{1,2,0:T(1,128)S(1)} %bitcast.108, f32[72,128,128]{2,1,0:T(8,128)} %param.15), kind=kOutput, calls=%fused_computation.109 | convolution fusion | flops 14155776 | bytes 4792320 | tf_op jit(solution)/shard_map/bij,bj->bi/dot_general | solution.py:93
  213.3 23.6 %psum.23 = f32[32,128]{1,0:T(8,128)S(1)} all-reduce(f32[32,128]{1,0:T(8,128)} %reduce-scatter.8.cloned.1.call-done), channel_id=1, replica_groups=mesh['rows'=8,'hub'=4] {'rows'}, use_global_device_ids=true, to_apply=%region_11.12 | all-reduce | flops 4096 | bytes 32768 | tf_op jit(solution)/shard_map/psum | solution.py:85
  236.9 0.6 multiply_subtract_fusion.3
  237.6 13.1 %all_gather.23 = f32[128,128]{1,0:T(8,128)S(1)} all-gather(f32[32,128]{1,0:T(8,128)S(1)} %get-tuple-element.3), channel_id=1, replica_groups=mesh['rows'=8,'hub'=4] {'hub'}, dimensions={0}, use_global_device_ids=true | all-gather | bytes 81920 | tf_op jit(solution)/shard_map/all_gather | solution.py:90
  250.7 0.6 gather_fusion.11
  251.2 2.5 fusion.63
  253.8 0.8 fusion.15
  (51 shorter events, 1.4 us)
Async XLA Ops:
  7.2 11.3 %copy-start = (f32[24,128,128]{2,1,0:T(8,128)S(1)}, f32[24,128,128]{2,1,0:T(8,128)}, u32[]{:S(2)}) copy-start(f32[24,128,128]{2,1,0:T(8,128)} %param.19) | copy-start | bytes 4718596
  7.2 34.5 %copy-start.7 = (f32[64,128]{1,0:T(8,128)S(1)}, f32[64,128]{1,0:T(8,128)}, u32[]{:S(2)}) copy-start(f32[64,128]{1,0:T(8,128)} %param.22) | copy-start | bytes 98308
  7.2 34.5 %copy-start.3 = (f32[64,128]{1,0:T(8,128)S(1)}, f32[64,128]{1,0:T(8,128)}, u32[]{:S(2)}) copy-start(f32[64,128]{1,0:T(8,128)} %param.23) | copy-start | bytes 98308
  7.2 34.5 %copy-start.2 = (f32[64,128]{1,0:T(8,128)S(1)}, f32[64,128]{1,0:T(8,128)}, u32[]{:S(2)}) copy-start(f32[64,128]{1,0:T(8,128)} %param.24) | copy-start | bytes 98308
  11.3 20.7 %all-to-all-start = ((s32[8,1,27]{2,1,0:T(1,128)}), s32[8,1,27]{2,1,0:T(1,128)S(1)}, u32[]{:S(2)}, u32[]{:S(2)}) async-start(s32[8,1,27]{2,1,0:T(1,128)} %all_to_all.15), calls=%async_computation | async-start | bytes 8192 | tf_op jit(solution)/shard_map/all_to_all | solution.py:43
  16.5 43.7 %reduce-scatter.4.cloned.1.call-start = ((), (), s32[]{:S(2)}) async-start(), calls=%async_computation.7 | async-start | bytes 81920 | tf_op jit(solution)/shard_map/reduce_scatter | solution.py:84
  24.7 35.4 %copy-start.10 = (s32[72]{0:T(128)S(1)}, s32[72]{0:T(128)}, u32[]{:S(2)}) copy-start(s32[72]{0:T(128)} %param.16) | copy-start | bytes 868
  24.7 59.2 %copy-start.4 = (f32[32,128]{1,0:T(8,128)S(1)}, f32[32,128]{1,0:T(8,128)}, u32[]{:S(2)}) copy-start(f32[32,128]{1,0:T(8,128)} %param.27) | copy-start | bytes 49156
  24.7 59.2 %copy-start.5 = (f32[32,128]{1,0:T(8,128)S(1)}, f32[32,128]{1,0:T(8,128)}, u32[]{:S(2)}) copy-start(f32[32,128]{1,0:T(8,128)} %param.26) | copy-start | bytes 49156
  24.7 59.2 %copy-start.8 = (f32[32,128]{1,0:T(8,128)S(1)}, f32[32,128]{1,0:T(8,128)}, u32[]{:S(2)}) copy-start(f32[32,128]{1,0:T(8,128)} %param.25) | copy-start | bytes 49156
  30.5 70.1 %copy-start.1 = (f32[16,128]{1,0:T(8,128)S(1)}, f32[16,128]{1,0:T(8,128)}, u32[]{:S(2)}) copy-start(f32[16,128]{1,0:T(8,128)} %param.28) | copy-start | bytes 24580
  30.5 70.1 %copy-start.6 = (f32[16,128]{1,0:T(8,128)S(1)}, f32[16,128]{1,0:T(8,128)}, u32[]{:S(2)}) copy-start(f32[16,128]{1,0:T(8,128)} %param.29) | copy-start | bytes 24580
  30.5 70.2 %copy-start.11 = (s32[24]{0:T(128)S(1)}, s32[24]{0:T(128)}, u32[]{:S(2)}) copy-start(s32[24]{0:T(128)} %param.20) | copy-start | bytes 292
  32.0 9.7 %all-to-all-start.1 = ((f32[8,27,128]{2,1,0:T(8,128)}), f32[8,27,128]{2,1,0:T(8,128)S(1)}, u32[]{:S(2)}, u32[]{:S(2)}) async-start(f32[8,27,128]{2,1,0:T(8,128)} %reshape.42), calls=%async_computation.1 | async-start | bytes 262144 | tf_op jit(solution)/shard_map/all_to_all | solution.py:63
  60.2 53.9 %copy-start.9 = (s32[24]{0:T(128)S(1)}, s32[24]{0:T(128)}, u32[]{:S(2)}) copy-start(s32[24]{0:T(128)} %param.21) | copy-start | bytes 292
  109.2 8.9 %all-to-all-start.2 = ((f32[8,27,128]{2,1,0:T(8,128)}), f32[8,27,128]{2,1,0:T(8,128)S(1)}, u32[]{:S(2)}, u32[]{:S(2)}) async-start(f32[8,27,128]{2,1,0:T(8,128)} %reshape.44), calls=%async_computation.3 | async-start | bytes 262144 | tf_op jit(solution)/shard_map/all_to_all | solution.py:63
  112.7 24.0 %reduce-scatter.6.cloned.1.call-start = ((), (), s32[]{:S(2)}) async-start(), calls=%async_computation.8 | async-start | bytes 81920 | tf_op jit(solution)/shard_map/reduce_scatter | solution.py:84
  185.3 8.9 %all-to-all-start.3 = ((f32[8,27,128]{2,1,0:T(8,128)}), f32[8,27,128]{2,1,0:T(8,128)S(1)}, u32[]{:S(2)}, u32[]{:S(2)}) async-start(f32[8,27,128]{2,1,0:T(8,128)} %reshape.46), calls=%async_computation.5 | async-start | bytes 262144 | tf_op jit(solution)/shard_map/all_to_all | solution.py:63
  188.7 24.6 %reduce-scatter.8.cloned.1.call-start = ((), (), s32[]{:S(2)}) async-start(), calls=%async_computation.9 | async-start | bytes 81920 | tf_op jit(solution)/shard_map/reduce_scatter | solution.py:84
Sparse Core Ops, SparseCore 0:
  21.5 20.9 reduce-scatter.3
  115.7 20.7 reduce-scatter.5
  191.8 20.7 reduce-scatter.7
where the time goes:
time: 262 us; the launch traced here: 261 us
  blocking collectives  136 us (52%)
  matrix products  62.6 us (24%)
  starting transfers between devices  16.3 us (6%)
  local copies, waits for them, and re-layouts  15 us (6%)
  between operations  14 us (5%)
  waiting for transfers between devices  10.7 us (4%)
  other arithmetic  6.44 us (2%)
    psum x3, blocking collectives, on_device(): hub_sums = lax.psum(hub_sums, 'rows')  70.9 us
    all_gather x3, blocking collectives, on_device(): hub_full = lax.all_gather(hub_extra, 'hub', axis=0, tiled=True)  40.1 us
    dot_general x3, matrix products, on_device(): jnp.einsum('bij,bj->bi', tail_blocks, tail_picked, precision=highest)  27.6 us
    all_gather x3, blocking collectives, on_device(): gathered = lax.all_gather(tail_extra, 'rows', axis=0, tiled=True)  25 us
    dot_general x3, matrix products, on_device(): jnp.einsum('bij,bi->bj', tail_blocks, duals[tail_row], precision=highest)  17.4 us
    all_to_all x3, starting transfers between devices, on_device(): lax.all_to_all(outgoing.reshape(row_devs, capacity, width), 'rows', split...  11 us
    all_to_all x3, waiting for transfers between devices, on_device(): lax.all_to_all(outgoing.reshape(row_devs, capacity, width), 'rows', split...  10.6 us
    dot_general x3, matrix products, on_device(): jnp.einsum('bij,bj->bi', hub_blocks, hub_full[hub_col], precision=highest)  7.63 us
  transfers between devices with their start and end apart: 7, of which 3 were waited for; matrix products, arithmetic and copies ran while one was open for 20% of the time, Pallas kernels for 0%

commit v1 on v0

--- a/solution.py
+++ b/solution.py
@@ -82,7 +82,7 @@
             hub_pick, hub_terms, precision=highest, preferred_element_type=jnp.float32
         )
         hub_sums = lax.psum_scatter(hub_partial, "hub", scatter_dimension=0, tiled=True)
-        hub_sums = lax.psum(hub_sums, "rows")
+        hub_sums = jnp.sum(lax.all_gather(hub_sums, "rows"), axis=0)
         hub_next = jnp.minimum(
             jnp.maximum(hub_state - primal_step * (cost_hub - hub_sums), 0.0), upper_hub
         )

time: 262 us -> 220 us (0.84)
  blocking collectives: 136 us -> 92.7 us
    psum x3 -> x0, blocking collectives: 70.9 us -> none  [on_device(): hub_sums = lax.psum(hub_sums, 'rows')]
    all_gather x0 -> x3, blocking collectives: none -> 27.6 us  [on_device(): hub_sums = jnp.sum(lax.all_gather(hub_sums, 'rows'), axis=0)]
  transfers between devices with their start and end apart: 7 -> 7, of which waited for: 3 -> 3; matrix products, arithmetic and copies ran while one was open for 20% -> 23% of each run, Pallas kernels for 0% -> 0%
where the time goes in v1:
time: 220 us; the launch traced here: 219 us
  blocking collectives  92.7 us (42%)
  matrix products  62.6 us (28%)
  starting transfers between devices  16.2 us (7%)
  local copies, waits for them, and re-layouts  15 us (7%)
  between operations  14 us (6%)
  waiting for transfers between devices  12 us (5%)
  other arithmetic  6.48 us (3%)
    all_gather x3, blocking collectives, on_device(): hub_full = lax.all_gather(hub_extra, 'hub', axis=0, tiled=True)  40 us
    all_gather x3, blocking collectives, on_device(): hub_sums = jnp.sum(lax.all_gather(hub_sums, 'rows'), axis=0)  27.6 us
    dot_general x3, matrix products, on_device(): jnp.einsum('bij,bj->bi', tail_blocks, tail_picked, precision=highest)  27.6 us
    all_gather x3, blocking collectives, on_device(): gathered = lax.all_gather(tail_extra, 'rows', axis=0, tiled=True)  25 us
    dot_general x3, matrix products, on_device(): jnp.einsum('bij,bi->bj', tail_blocks, duals[tail_row], precision=highest)  17.4 us
    all_to_all x3, waiting for transfers between devices, on_device(): lax.all_to_all(outgoing.reshape(row_devs, capacity, width), 'rows', split...  11.9 us
    all_to_all x3, starting transfers between devices, on_device(): lax.all_to_all(outgoing.reshape(row_devs, capacity, width), 'rows', split...  10.9 us
    dot_general x3, matrix products, on_device(): jnp.einsum('bij,bj->bi', hub_blocks, hub_full[hub_col], precision=highest)  7.63 us
  transfers between devices with their start and end apart: 7, of which 3 were waited for; matrix products, arithmetic and copies ran while one was open for 23% of the time, Pallas kernels for 0%

profile of v1, /device:TPU:0, one launch (start us, length us, event | category | flops | bytes accessed | tf_op | source)
XLA Modules:
  0.0 219.0 jit_solution(322656416827709993)
XLA Ops:
  7.2 0.8 fusion.33
  8.2 0.8 select_reduce_fusion
  9.0 0.7 fusion.49
  9.7 0.9 scatter_custom_fusion
  10.6 0.7 all_to_all.15
  11.3 5.2 %all-to-all-start = ((s32[8,1,27]{2,1,0:T(1,128)}), s32[8,1,27]{2,1,0:T(1,128)S(1)}, u32[]{:S(2)}, u32[]{:S(2)}) async-start(s32[8,1,27]{2,1,0:T(1,128)} %all_to_all.15), calls=%async_computation | async-start | bytes 8192 | tf_op jit(solution)/shard_map/all_to_all | solution.py:43
  16.5 0.7 compare_select_fusion.1
  17.2 1.3 gather_fusion.2
  18.5 1.4 fusion.54
  19.9 1.5 fusion.26
  21.4 0.7 compare_select_fusion.2
  22.1 0.7 compare_select_fusion
  22.7 0.7 compare_select_fusion.3
  23.4 1.3 gather_fusion
  24.7 5.8 %fusion.52 = f32[72,1,128]{2,1,0:T(1,128)S(1)} fusion(f32[72,128,1]{1,2,0:T(1,128)S(1)} %bitcast.118, f32[72,128,128]{2,1,0:T(8,128)} %param.15), kind=kOutput, calls=%fused_computation.99 | convolution fusion | flops 14155776 | bytes 4792320 | tf_op jit(solution)/shard_map/bij,bi->bj/dot_general | solution.py:61
  30.6 0.8 scatter_custom_fusion.1
  31.3 0.7 reshape.42
  32.0 4.2 %all-to-all-start.1 = ((f32[8,27,128]{2,1,0:T(8,128)}), f32[8,27,128]{2,1,0:T(8,128)S(1)}, u32[]{:S(2)}, u32[]{:S(2)}) async-start(f32[8,27,128]{2,1,0:T(8,128)} %reshape.42), calls=%async_computation.1 | async-start | bytes 262144 | tf_op jit(solution)/shard_map/all_to_all | solution.py:63
  36.2 0.5 broadcast.172
  36.7 0.7 reduce.3
  37.4 4.2 %all-to-all-done.1 = f32[8,27,128]{2,1,0:T(8,128)S(1)} async-done(((f32[8,27,128]{2,1,0:T(8,128)}), f32[8,27,128]{2,1,0:T(8,128)S(1)}, u32[]{:S(2)}, u32[]{:S(2)}) %all-to-all-start.1) | async-done | bytes 110624 | tf_op jit(solution)/shard_map/all_to_all | solution.py:63
  41.7 0.2 multiply_subtract_fusion.2
  41.9 8.4 %all_gather.36 = f32[512,128]{1,0:T(8,128)S(1)} all-gather(f32[64,128]{1,0:T(8,128)S(1)} %get-tuple-element.9), channel_id=1, replica_groups=mesh['rows'=8,'hub'=4] {'rows'}, dimensions={0}, use_global_device_ids=true | all-gather | bytes 294912 | tf_op jit(solution)/shard_map/all_gather | solution.py:91
  50.3 0.6 gather_fusion.1
  50.9 9.2 %fusion.53 = f32[72,1,128]{2,1,0:T(1,128)S(1)} fusion(f32[72,128,1]{1,2,0:T(1,128)S(1)} %bitcast.115, f32[72,128,128]{2,1,0:T(8,128)} %param.15), kind=kOutput, calls=%fused_computation.100 | convolution fusion | flops 14155776 | bytes 4792320 | tf_op jit(solution)/shard_map/bij,bj->bi/dot_general | solution.py:93
  60.2 9.2 %all-gather = f32[256,128]{1,0:T(8,128)S(1)} all-gather(f32[32,128]{1,0:T(8,128)} %reduce-scatter.4.cloned.1.call-done), channel_id=2, replica_groups=mesh['rows'=8,'hub'=4] {'rows'}, dimensions={0}, use_global_device_ids=true | all-gather | bytes 147456 | tf_op jit(solution)/shard_map/all_gather | solution.py:85
  69.4 13.5 %all_gather.39 = f32[128,128]{1,0:T(8,128)S(1)} all-gather(f32[32,128]{1,0:T(8,128)S(1)} %get-tuple-element.7), channel_id=1, replica_groups=mesh['rows'=8,'hub'=4] {'hub'}, dimensions={0}, use_global_device_ids=true | all-gather | bytes 81920 | tf_op jit(solution)/shard_map/all_gather | solution.py:90
  83.0 0.6 gather_fusion.3
  83.5 2.5 %fusion.55 = f32[24,1,128]{2,1,0:T(1,128)S(1)} fusion(f32[24,128,1]{1,2,0:T(1,128)S(1)} %bitcast.124, f32[24,128,128]{2,1,0:T(8,128)S(1)} %copy-done), kind=kOutput, calls=%fused_computation.102 | convolution fusion | flops 4718592 | bytes 1597440 | tf_op jit(solution)/shard_map/bij,bj->bi/dot_general | solution.py:94
  86.2 0.6 gather_fusion.4
  86.8 0.6 gather_fusion.6
  87.4 5.8 %fusion.56 = f32[72,1,128]{2,1,0:T(1,128)S(1)} fusion(f32[72,128,1]{1,2,0:T(1,128)S(1)} %bitcast.116, f32[72,128,128]{2,1,0:T(8,128)} %param.15), kind=kOutput, calls=%fused_computation.103 | convolution fusion | flops 14155776 | bytes 4792320 | tf_op jit(solution)/shard_map/bij,bi->bj/dot_general | solution.py:61
  93.2 0.8 scatter_custom_fusion.2
  94.0 0.7 reshape.44
  94.6 3.4 %all-to-all-start.2 = ((f32[8,27,128]{2,1,0:T(8,128)}), f32[8,27,128]{2,1,0:T(8,128)S(1)}, u32[]{:S(2)}, u32[]{:S(2)}) async-start(f32[8,27,128]{2,1,0:T(8,128)} %reshape.44), calls=%async_computation.3 | async-start | bytes 262144 | tf_op jit(solution)/shard_map/all_to_all | solution.py:63
  98.1 1.4 fusion.58
  99.5 0.8 fusion.25
  100.3 3.1 %all-to-all-done.2 = f32[8,27,128]{2,1,0:T(8,128)S(1)} async-done(((f32[8,27,128]{2,1,0:T(8,128)}), f32[8,27,128]{2,1,0:T(8,128)S(1)}, u32[]{:S(2)}, u32[]{:S(2)}) %all-to-all-start.2) | async-done | bytes 110624 | tf_op jit(solution)/shard_map/all_to_all | solution.py:63
  103.7 8.3 %all_gather.40 = f32[512,128]{1,0:T(8,128)S(1)} all-gather(f32[64,128]{1,0:T(8,128)S(1)} %get-tuple-element.11), channel_id=1, replica_groups=mesh['rows'=8,'hub'=4] {'rows'}, dimensions={0}, use_global_device_ids=true | all-gather | bytes 294912 | tf_op jit(solution)/shard_map/all_gather | solution.py:91
  112.0 0.6 gather_fusion.5
  112.6 9.2 %fusion.57 = f32[72,1,128]{2,1,0:T(1,128)S(1)} fusion(f32[72,128,1]{1,2,0:T(1,128)S(1)} %bitcast.117, f32[72,128,128]{2,1,0:T(8,128)} %param.15), kind=kOutput, calls=%fused_computation.104 | convolution fusion | flops 14155776 | bytes 4792320 | tf_op jit(solution)/shard_map/bij,bj->bi/dot_general | solution.py:93
  122.0 9.3 %all-gather.1 = f32[256,128]{1,0:T(8,128)S(1)} all-gather(f32[32,128]{1,0:T(8,128)} %reduce-scatter.6.cloned.1.call-done), channel_id=3, replica_groups=mesh['rows'=8,'hub'=4] {'rows'}, dimensions={0}, use_global_device_ids=true | all-gather | bytes 147456 | tf_op jit(solution)/shard_map/all_gather | solution.py:85
  131.3 13.4 %all_gather.43 = f32[128,128]{1,0:T(8,128)S(1)} all-gather(f32[32,128]{1,0:T(8,128)S(1)} %get-tuple-element.5), channel_id=1, replica_groups=mesh['rows'=8,'hub'=4] {'hub'}, dimensions={0}, use_global_device_ids=true | all-gather | bytes 81920 | tf_op jit(solution)/shard_map/all_gather | solution.py:90
  144.6 0.6 gather_fusion.7
  145.2 2.5 %fusion.59 = f32[24,1,128]{2,1,0:T(1,128)S(1)} fusion(f32[24,128,1]{1,2,0:T(1,128)S(1)} %bitcast.126, f32[24,128,128]{2,1,0:T(8,128)S(1)} %copy-done), kind=kOutput, calls=%fused_computation.106 | convolution fusion | flops 4718592 | bytes 1597440 | tf_op jit(solution)/shard_map/bij,bj->bi/dot_general | solution.py:94
  147.9 0.6 gather_fusion.9
  148.5 0.6 gather_fusion.8
  149.1 1.4 fusion.61
  150.5 5.8 %fusion.60 = f32[72,1,128]{2,1,0:T(1,128)S(1)} fusion(f32[72,128,1]{1,2,0:T(1,128)S(1)} %bitcast.113, f32[72,128,128]{2,1,0:T(8,128)} %param.15), kind=kOutput, calls=%fused_computation.107 | convolution fusion | flops 14155776 | bytes 4792320 | tf_op jit(solution)/shard_map/bij,bi->bj/dot_general | solution.py:61
  156.3 0.8 scatter_custom_fusion.3
  157.1 0.7 reshape.46
  157.7 3.4 %all-to-all-start.3 = ((f32[8,27,128]{2,1,0:T(8,128)}), f32[8,27,128]{2,1,0:T(8,128)S(1)}, u32[]{:S(2)}, u32[]{:S(2)}) async-start(f32[8,27,128]{2,1,0:T(8,128)} %reshape.46), calls=%async_computation.5 | async-start | bytes 262144 | tf_op jit(solution)/shard_map/all_to_all | solution.py:63
  161.2 0.8 fusion.24
  162.0 4.6 %all-to-all-done.3 = f32[8,27,128]{2,1,0:T(8,128)S(1)} async-done(((f32[8,27,128]{2,1,0:T(8,128)}), f32[8,27,128]{2,1,0:T(8,128)S(1)}, u32[]{:S(2)}, u32[]{:S(2)}) %all-to-all-start.3) | async-done | bytes 110624 | tf_op jit(solution)/shard_map/all_to_all | solution.py:63
  166.6 0.8 multiply_subtract_fusion
  167.4 8.3 %all_gather.46 = f32[512,128]{1,0:T(8,128)S(1)} all-gather(f32[64,128]{1,0:T(8,128)S(1)} %get-tuple-element.13), channel_id=1, replica_groups=mesh['rows'=8,'hub'=4] {'rows'}, dimensions={0}, use_global_device_ids=true | all-gather | bytes 294912 | tf_op jit(solution)/shard_map/all_gather | solution.py:91
  175.7 0.6 gather_fusion.10
  176.3 9.2 %fusion.62 = f32[72,1,128]{2,1,0:T(1,128)S(1)} fusion(f32[72,128,1]{1,2,0:T(1,128)S(1)} %bitcast.114, f32[72,128,128]{2,1,0:T(8,128)} %param.15), kind=kOutput, calls=%fused_computation.109 | convolution fusion | flops 14155776 | bytes 4792320 | tf_op jit(solution)/shard_map/bij,bj->bi/dot_general | solution.py:93
  185.6 9.2 %all-gather.2 = f32[256,128]{1,0:T(8,128)S(1)} all-gather(f32[32,128]{1,0:T(8,128)} %reduce-scatter.8.cloned.1.call-done), channel_id=4, replica_groups=mesh['rows'=8,'hub'=4] {'rows'}, dimensions={0}, use_global_device_ids=true | all-gather | bytes 147456 | tf_op jit(solution)/shard_map/all_gather | solution.py:85
  194.8 0.6 multiply_subtract_fusion.3
  195.5 13.1 %all_gather.47 = f32[128,128]{1,0:T(8,128)S(1)} all-gather(f32[32,128]{1,0:T(8,128)S(1)} %get-tuple-element.3), channel_id=1, replica_groups=mesh['rows'=8,'hub'=4] {'hub'}, dimensions={0}, use_global_device_ids=true | all-gather | bytes 81920 | tf_op jit(solution)/shard_map/all_gather | solution.py:90
  208.6 0.6 gather_fusion.11
  209.1 2.5 %fusion.63 = f32[24,1,128]{2,1,0:T(1,128)S(1)} fusion(f32[24,128,1]{1,2,0:T(1,128)S(1)} %bitcast.122, f32[24,128,128]{2,1,0:T(8,128)S(1)} %copy-done), kind=kOutput, calls=%fused_computation.110 | convolution fusion | flops 4718592 | bytes 1597440 | tf_op jit(solution)/shard_map/bij,bj->bi/dot_general | solution.py:94
  211.7 0.8 fusion.15
  (54 shorter events, 1.5 us)
Async XLA Ops:
  7.2 11.3 %copy-start = (f32[24,128,128]{2,1,0:T(8,128)S(1)}, f32[24,128,128]{2,1,0:T(8,128)}, u32[]{:S(2)}) copy-start(f32[24,128,128]{2,1,0:T(8,128)} %param.19) | copy-start | bytes 4718596
  7.2 34.5 %copy-start.7 = (f32[64,128]{1,0:T(8,128)S(1)}, f32[64,128]{1,0:T(8,128)}, u32[]{:S(2)}) copy-start(f32[64,128]{1,0:T(8,128)} %param.22) | copy-start | bytes 98308
  7.2 34.5 %copy-start.3 = (f32[64,128]{1,0:T(8,128)S(1)}, f32[64,128]{1,0:T(8,128)}, u32[]{:S(2)}) copy-start(f32[64,128]{1,0:T(8,128)} %param.23) | copy-start | bytes 98308
  7.2 34.5 %copy-start.2 = (f32[64,128]{1,0:T(8,128)S(1)}, f32[64,128]{1,0:T(8,128)}, u32[]{:S(2)}) copy-start(f32[64,128]{1,0:T(8,128)} %param.24) | copy-start | bytes 98308
  11.3 20.7 %all-to-all-start = ((s32[8,1,27]{2,1,0:T(1,128)}), s32[8,1,27]{2,1,0:T(1,128)S(1)}, u32[]{:S(2)}, u32[]{:S(2)}) async-start(s32[8,1,27]{2,1,0:T(1,128)} %all_to_all.15), calls=%async_computation | async-start | bytes 8192 | tf_op jit(solution)/shard_map/all_to_all | solution.py:43
  16.5 43.7 %reduce-scatter.4.cloned.1.call-start = ((), (), s32[]{:S(2)}) async-start(), calls=%async_computation.7 | async-start | bytes 81920 | tf_op jit(solution)/shard_map/reduce_scatter | solution.py:84
  24.7 35.4 %copy-start.10 = (s32[72]{0:T(128)S(1)}, s32[72]{0:T(128)}, u32[]{:S(2)}) copy-start(s32[72]{0:T(128)} %param.16) | copy-start | bytes 868
  24.7 44.7 %copy-start.4 = (f32[32,128]{1,0:T(8,128)S(1)}, f32[32,128]{1,0:T(8,128)}, u32[]{:S(2)}) copy-start(f32[32,128]{1,0:T(8,128)} %param.27) | copy-start | bytes 49156
  24.7 44.7 %copy-start.5 = (f32[32,128]{1,0:T(8,128)S(1)}, f32[32,128]{1,0:T(8,128)}, u32[]{:S(2)}) copy-start(f32[32,128]{1,0:T(8,128)} %param.26) | copy-start | bytes 49156
  24.7 44.7 %copy-start.8 = (f32[32,128]{1,0:T(8,128)S(1)}, f32[32,128]{1,0:T(8,128)}, u32[]{:S(2)}) copy-start(f32[32,128]{1,0:T(8,128)} %param.25) | copy-start | bytes 49156
  30.5 55.6 %copy-start.1 = (f32[16,128]{1,0:T(8,128)S(1)}, f32[16,128]{1,0:T(8,128)}, u32[]{:S(2)}) copy-start(f32[16,128]{1,0:T(8,128)} %param.28) | copy-start | bytes 24580
  30.5 55.6 %copy-start.6 = (f32[16,128]{1,0:T(8,128)S(1)}, f32[16,128]{1,0:T(8,128)}, u32[]{:S(2)}) copy-start(f32[16,128]{1,0:T(8,128)} %param.29) | copy-start | bytes 24580
  30.5 55.6 %copy-start.11 = (s32[24]{0:T(128)S(1)}, s32[24]{0:T(128)}, u32[]{:S(2)}) copy-start(s32[24]{0:T(128)} %param.20) | copy-start | bytes 292
  32.0 9.7 %all-to-all-start.1 = ((f32[8,27,128]{2,1,0:T(8,128)}), f32[8,27,128]{2,1,0:T(8,128)S(1)}, u32[]{:S(2)}, u32[]{:S(2)}) async-start(f32[8,27,128]{2,1,0:T(8,128)} %reshape.42), calls=%async_computation.1 | async-start | bytes 262144 | tf_op jit(solution)/shard_map/all_to_all | solution.py:63
  69.4 30.1 %copy-start.9 = (s32[24]{0:T(128)S(1)}, s32[24]{0:T(128)}, u32[]{:S(2)}) copy-start(s32[24]{0:T(128)} %param.21) | copy-start | bytes 292
  94.6 8.8 %all-to-all-start.2 = ((f32[8,27,128]{2,1,0:T(8,128)}), f32[8,27,128]{2,1,0:T(8,128)S(1)}, u32[]{:S(2)}, u32[]{:S(2)}) async-start(f32[8,27,128]{2,1,0:T(8,128)} %reshape.44), calls=%async_computation.3 | async-start | bytes 262144 | tf_op jit(solution)/shard_map/all_to_all | solution.py:63
  98.0 23.9 %reduce-scatter.6.cloned.1.call-start = ((), (), s32[]{:S(2)}) async-start(), calls=%async_computation.8 | async-start | bytes 81920 | tf_op jit(solution)/shard_map/reduce_scatter | solution.py:84
  157.7 8.8 %all-to-all-start.3 = ((f32[8,27,128]{2,1,0:T(8,128)}), f32[8,27,128]{2,1,0:T(8,128)S(1)}, u32[]{:S(2)}, u32[]{:S(2)}) async-start(f32[8,27,128]{2,1,0:T(8,128)} %reshape.46), calls=%async_computation.5 | async-start | bytes 262144 | tf_op jit(solution)/shard_map/all_to_all | solution.py:63
  161.1 24.5 %reduce-scatter.8.cloned.1.call-start = ((), (), s32[]{:S(2)}) async-start(), calls=%async_computation.9 | async-start | bytes 81920 | tf_op jit(solution)/shard_map/reduce_scatter | solution.py:84
Sparse Core Ops, SparseCore 0:
  21.5 20.9 reduce-scatter.3
  101.1 20.6 reduce-scatter.5
  164.2 20.6 reduce-scatter.7
